TPU v7x, 256 devices: a whole 4x4x8 slice. The times are simulated.
256 devices in a mesh: row: 8 (over x, core), col: 32 (over y, z).
Axes of the slice: x: 4, y: 4, z: 8, core: 2. Of those that a mesh axis runs over, the one named last changes fastest.
Arguments:
- pooled: bfloat16 [16384, 1152], P(('row', 'col')), may hold values from -32 to 32
- hidden: bfloat16 [16384, 4304], P(('row', 'col')), may hold values from -6 to 6
- text: bfloat16 [16384, 1152], P(('row', 'col')), may hold values from -12 to 12
- weight: float32 [1152, 4304], P('col', 'row'), may hold values from -0.09375 to 0.09375
- row_moment: float32 [1152], P('col'), may hold values from 1e-07 to 1e-05
- col_moment: float32 [4304], P('row'), may hold values from 1e-07 to 1e-05
- log_scale: float32 [], replicated, may hold values from 4.2 to 4.8
- bias: float32 [], replicated, may hold values from -16 to -12
Outputs:
- update: float32 [1152, 4304], P('col', 'row')
- new_row: float32 [1152], P('col')
- new_col: float32 [4304], P('row')
- loss: float32 [], replicated
All inputs are finite; a program needn't handle non-finite values.
Results may differ from a plain program's by a relative error of at most 0.004.
Values may be sent and summed in bfloat16 or wider, within the bound.
No kernel may reach another device: no remote copies, remote signals or barrier semaphores. Data moves between devices by JAX's collectives and lax.ppermute only.
A program may use at most 128 MiB of HBM per device.

v0:
```python
import functools
import jax
import jax.numpy as jnp
from jax import lax
from jax.sharding import Mesh
from jax.sharding import PartitionSpec as P

D = 1152
FF = 4304
ROW = ("row_0", "row_1")
COL = ("col_0", "col_1")
ROW_COL = ("row_0", "row_1", "col_0", "col_1")
EPSILON = 1e-06
DECAY_RATE = 0.8
CLIP_LEVEL = 1.0
FLOOR_VALUE = 1e-30


def laid_out(pieces, dim):
    dims = list(pieces.shape[1:])
    dims[dim] *= pieces.shape[0]
    return jnp.moveaxis(pieces, 0, dim).reshape(dims)


def sent_to_all(array, axis):
    copies = jnp.broadcast_to(array, (lax.axis_size(axis), *array.shape))
    return lax.all_to_all(copies, axis, split_axis=0, concat_axis=0, tiled=True)


def collect(array, axis, dim):
    return laid_out(sent_to_all(array, axis), dim)


def split_up(array, dim, devices):
    dims = array.shape
    pieces = array.reshape(*dims[:dim], devices, dims[dim] // devices, *dims[dim + 1 :])
    return jnp.moveaxis(pieces, dim, 0)


def sum_at_owner(array, axis, dim):
    pieces = split_up(array, dim, lax.axis_size(axis))
    arrived = lax.all_to_all(pieces, axis, split_axis=0, concat_axis=0, tiled=True)
    return arrived.sum(axis=0)


def sum_by_axis(running, axes):
    for axis in axes:
        running = lax.psum_scatter(running, axis, scatter_dimension=0, tiled=True)
    return running


def of_everyone(array, axis):
    everything = sent_to_all(array, axis)
    return jnp.sum(everything, axis=0)


def one_axis_at_a_time(array, axes):
    return functools.reduce(lax.psum, axes, array)


def over_row_index(positions, column, tokens, columns):
    return (positions // tokens * columns + column) * tokens + positions % tokens


def over_col_index(positions, row_place, tokens, columns):
    return row_place * columns * tokens + positions


def pair_tile(images, image_ids, texts, text_ids, logit_scale, bias, batch_total):
    logits = logit_scale * jnp.dot(images, texts.T, preferred_element_type=jnp.float32) + bias
    label_sign = jnp.where(
        image_ids[:, None] == text_ids[None, :], jnp.float32(1.0), jnp.float32(-1.0)
    )
    loss_sum = jnp.sum(jax.nn.softplus(-label_sign * logits))
    grad_logits = (-label_sign * jax.nn.sigmoid(-label_sign * logits) / batch_total).astype(
        jnp.bfloat16
    )
    return (loss_sum, logit_scale * jnp.dot(grad_logits, texts, preferred_element_type=jnp.float32))


def per_device(pooled, hidden, text, weight, row_moment, col_moment, log_scale, bias):
    rows_count = lax.axis_size(ROW)
    cols_count = lax.axis_size(COL)
    row_place = lax.axis_index(ROW)
    col_place = lax.axis_index(COL)
    tokens = pooled.shape[0]
    batch_total = tokens * rows_count * cols_count
    split_hidden = lax.all_to_all(hidden, ROW, split_axis=1, concat_axis=0, tiled=True)
    weight_half = weight.astype(jnp.bfloat16)
    partial_proj = lax.dot_general(
        split_hidden,
        collect(weight_half, COL, 0),
        (((1,), (1,)), ((), ())),
        preferred_element_type=jnp.float32,
    )
    projected = sum_at_owner(partial_proj, ROW, 0)
    mixed_rows = pooled.astype(jnp.float32) + projected
    length = jnp.sqrt(jnp.sum(mixed_rows * mixed_rows, axis=1, keepdims=True) + EPSILON)
    image_unit = mixed_rows / length
    images = image_unit.astype(jnp.bfloat16)
    text_float = text.astype(jnp.float32)
    text_units = (
        text_float / jnp.sqrt(jnp.sum(text_float * text_float, axis=1, keepdims=True) + EPSILON)
    ).astype(jnp.bfloat16)
    logit_scale = jnp.exp(log_scale)
    image_rows = collect(images, ROW, 0)
    image_ids = over_row_index(
        jnp.arange(image_rows.shape[0], dtype=jnp.int32), col_place, tokens, cols_count
    )
    piece = lax.all_gather(text_units, COL, axis=0, tiled=True)
    text_ids = over_col_index(
        jnp.arange(piece.shape[0], dtype=jnp.int32), row_place, tokens, cols_count
    )
    loss_local, unit_part = pair_tile(
        image_rows, image_ids, piece, text_ids, logit_scale, bias, batch_total
    )
    unit_grad = sum_at_owner(unit_part, ROW, 0)
    mixed_grad = (
        (unit_grad - image_unit * jnp.sum(image_unit * unit_grad, axis=1, keepdims=True)) / length
    ).astype(jnp.bfloat16)
    grad_rows = collect(mixed_grad, ROW, 0)
    gradient = sum_by_axis(
        lax.dot_general(
            grad_rows, split_hidden, (((0,), (0,)), ((), ())), preferred_element_type=jnp.float32
        ),
        COL,
    )
    squared = gradient * gradient + FLOOR_VALUE
    row_sum = of_everyone(jnp.sum(squared, axis=1), ROW)
    col_sum = of_everyone(jnp.sum(squared, axis=0), COL)
    new_row = DECAY_RATE * row_moment + (1.0 - DECAY_RATE) * row_sum / FF
    new_col = DECAY_RATE * col_moment + (1.0 - DECAY_RATE) * col_sum / D
    second = new_row[:, None] * new_col[None, :]
    raw_update = gradient / jnp.sqrt(second)
    loss_total, update_total = (
        one_axis_at_a_time(loss_local, ROW_COL),
        one_axis_at_a_time(jnp.sum(raw_update * raw_update), ROW_COL),
    )
    update_rms = jnp.sqrt(update_total / (D * FF))
    update = raw_update / jnp.maximum(1.0, update_rms / CLIP_LEVEL)
    loss = loss_total / batch_total
    return (update, new_row, new_col, loss)


def solution(mesh):
    finer = Mesh(mesh.devices.reshape(4, 2, 4, 8), ("row_0", "row_1", "col_0", "col_1"))
    return jax.shard_map(
        per_device,
        mesh=finer,
        in_specs=(
            P(ROW_COL, None),
            P(ROW_COL, None),
            P(ROW_COL, None),
            P(COL, ROW),
            P(COL),
            P(ROW),
            P(),
            P(),
        ),
        out_specs=(P(COL, ROW), P(COL), P(ROW), P()),
        check_vma=False,
    )
```

profile of v0, /device:TPU:2, one launch (start us, length us, event | category | flops | bytes accessed | tf_op | source)
XLA Modules:
  0.0 357.6 jit_solution(11246897454921141489)
XLA Ops:
  7.2 0.0 all-gather.2.cloned.1.call-start
  7.2 1.1 fusion.10
  8.3 1.7 fusion.11
  10.0 0.9 convert_element_type.22
  10.9 1.3 broadcast_in_dim.32
  12.2 11.5 %all-to-all-start.1 = ((bf16[32,36,538]{2,1,0:T(8,128)(2,1)}), bf16[32,36,538]{2,1,0:T(8,128)(2,1)S(1)}, u32[]{:S(2)}, u32[]{:S(2)}) async-start(bf16[32,36,538]{2,1,0:T(8,128)(2,1)} %broadcast_in_dim.32), calls=%async_computation.1 | async-start | bytes 3276800 | tf_op jit(solution)/shard_map/all_to_all | solution.py:27
  23.8 0.8 all_to_all.35
  24.5 0.9 copy.19
  25.5 44.5 %all-to-all-done.1 = bf16[32,36,538]{2,1,0:T(8,128)(2,1)S(1)} async-done(((bf16[32,36,538]{2,1,0:T(8,128)(2,1)}), bf16[32,36,538]{2,1,0:T(8,128)(2,1)S(1)}, u32[]{:S(2)}, u32[]{:S(2)}) %all-to-all-start.1) | async-done | bytes 1239584 | tf_op jit(solution)/shard_map/all_to_all | solution.py:27
  69.9 4.8 %all-to-all-start = ((bf16[64,8,538]{2,0,1:T(8,128)(2,1)}), bf16[64,8,538]{2,0,1:T(8,128)(2,1)}, u32[]{:S(2)}, u32[]{:S(2)}) async-start(bf16[64,8,538]{2,0,1:T(8,128)(2,1)} %copy.19), calls=%async_computation | async-start | bytes 1310720 | tf_op jit(solution)/shard_map/all_to_all | solution.py:88
  74.8 0.6 reshape.75
  75.4 9.7 %all-to-all-done = bf16[64,8,538]{2,0,1:T(8,128)(2,1)} async-done(((bf16[64,8,538]{2,0,1:T(8,128)(2,1)}), bf16[64,8,538]{2,0,1:T(8,128)(2,1)}, u32[]{:S(2)}, u32[]{:S(2)}) %all-to-all-start) | async-done | bytes 550944 | tf_op jit(solution)/shard_map/all_to_all | solution.py:88
  85.1 2.3 fusion.6
  87.5 32.9 %all_to_all.53 = f32[8,64,1152]{2,1,0:T(8,128)S(1)} all-to-all(f32[8,64,1152]{2,1,0:T(8,128)S(1)} %fusion.6), channel_id=1, replica_groups=mesh['row_0'=4,'row_1'=2,'col_0'=4,'col_1'=8] {'row_0','row_1'}, dimensions={0} | all-to-all | bytes 4718592 | tf_op jit(solution)/shard_map/all_to_all | solution.py:42
  120.4 0.1 reduce_sum.99
  120.5 0.1 multiply_reduce_fusion.1
  120.7 0.1 fusion.30
  120.8 1.2 broadcast_in_dim.33
  122.0 4.7 %all-to-all-start.3 = ((bf16[8,64,1152]{2,1,0:T(8,128)(2,1)}), bf16[8,64,1152]{2,1,0:T(8,128)(2,1)S(1)}, u32[]{:S(2)}, u32[]{:S(2)}) async-start(bf16[8,64,1152]{2,1,0:T(8,128)(2,1)} %broadcast_in_dim.33), calls=%async_computation.3 | async-start | bytes 2359296 | tf_op jit(solution)/shard_map/all_to_all | solution.py:27
  128.0 14.5 %all-to-all-done.3 = bf16[8,64,1152]{2,1,0:T(8,128)(2,1)S(1)} async-done(((bf16[8,64,1152]{2,1,0:T(8,128)(2,1)}), bf16[8,64,1152]{2,1,0:T(8,128)(2,1)S(1)}, u32[]{:S(2)}, u32[]{:S(2)}) %all-to-all-start.3) | async-done | bytes 1179680 | tf_op jit(solution)/shard_map/all_to_all | solution.py:27
  142.5 8.2 %fusion.1 = (f32[]{:T(128)}, f32[512,2048]{1,0:T(8,128)S(1)}) fusion(f32[]{:T(128)S(6)} %copy.27, bf16[512,1152]{1,0:T(8,128)(2,1)S(1)} %bitcast.21, bf16[2048,1152]{1,0:T(8,128)(2,1)} %all-gather.2.cloned.1.call-done, f32[]{:T(128)S(6)} %exp.10, s32[2048]{0:T(1024)S(1)} %iota_add_fusion, s32[512]{0:T(512)S(1)} %fusion.23), kind=kOutput, calls=%fused_computation.1 | convolution fusion | flops 2429550592 | bytes 10102796 | tf_op jit(solution)/shard_map/dot_general | solution.py:70
  150.8 3.7 %convolution_multiply_fusion = f32[512,1152]{1,0:T(8,128)S(1)} fusion(bf16[2048,1152]{1,0:T(8,128)(2,1)S(1)} %copy-done.6, f32[512,2048]{1,0:T(8,128)S(1)} %get-tuple-element.15, s32[2048]{0:T(1024)S(1)} %iota_add_fusion, s32[512]{0:T(512)S(1)} %fusion.23, f32[]{:T(128)S(6)} %exp.10), kind=kOutput, calls=%fused_computation.6 | convolution fusion | flops 2425946112 | bytes 11282436 | tf_op jit(solution)/shard_map/dot_general | solution.py:78
  154.5 32.7 %all_to_all.54 = f32[8,64,1152]{2,1,0:T(8,128)S(1)} all-to-all(f32[8,64,1152]{2,1,0:T(8,128)S(1)} %bitcast.20), channel_id=1, replica_groups=mesh['row_0'=4,'row_1'=2,'col_0'=4,'col_1'=8] {'row_0','row_1'}, dimensions={0} | all-to-all | bytes 4718592 | tf_op jit(solution)/shard_map/all_to_all | solution.py:42
  187.2 0.1 reduce_sum.102
  187.3 0.2 multiply_reduce_fusion
  187.5 0.1 divide_convert_fusion
  187.7 0.1 broadcast_in_dim.34
  187.8 19.6 %all_to_all.55 = bf16[8,64,1152]{2,1,0:T(8,128)(2,1)S(1)} all-to-all(bf16[8,64,1152]{2,1,0:T(8,128)(2,1)S(1)} %broadcast_in_dim.34), channel_id=1, replica_groups=mesh['row_0'=4,'row_1'=2,'col_0'=4,'col_1'=8] {'row_0','row_1'}, dimensions={0} | all-to-all | bytes 2359296 | tf_op jit(solution)/shard_map/all_to_all | solution.py:27
  207.4 3.8 %convolution_bitcast_fusion = f32[1152,538]{1,0:T(8,128)} fusion(bf16[8,64,1152]{2,1,0:T(8,128)(2,1)S(1)} %all_to_all.55, bf16[64,8,538]{2,0,1:T(8,128)(2,1)} %all-to-all-done), kind=kOutput, calls=%fused_computation.5 | convolution fusion | flops 634650624 | bytes 4209664 | tf_op jit(solution)/shard_map/dot_general | solution.py:123
  211.2 35.5 %reduce-scatter.4.cloned.1.call-done = f32[288,538]{1,0:T(8,128)} async-done(((f32[1152,538]{1,0:T(8,128)}), f32[288,538]{1,0:T(8,128)}) %reduce-scatter.4.cloned.1.call-update) | async-done | bytes 619792 | tf_op jit(solution)/shard_map/reduce_scatter | solution.py:48
  246.7 23.8 %fusion = f32[48,538]{1,0:T(8,128)S(1)} fusion(f32[288,538]{1,0:T(8,128)} %reduce-scatter.4.cloned.1.call-done), kind=kCustom, calls=%all-reduce-scatter | all-reduce-scatter fusion | flops 206593 | bytes 724096
  270.5 2.8 collective-permute-start
  273.3 2.4 collective-permute-start.1
  275.7 0.6 dynamic-slice.4
  277.0 1.0 collective-permute-done.1
  278.0 0.4 concatenate
  278.4 0.1 fusion.14
  278.5 8.4 %all_to_all.56 = f32[8,1,36]{2,1,0:T(1,128)S(1)} all-to-all(f32[8,1,36]{2,1,0:T(1,128)S(1)} %broadcast_in_dim.35), channel_id=1, replica_groups=mesh['row_0'=4,'row_1'=2,'col_0'=4,'col_1'=8] {'row_0','row_1'}, dimensions={0} | all-to-all | bytes 2304 | tf_op jit(solution)/shard_map/all_to_all | solution.py:27
  286.9 0.7 broadcast_in_dim.36
  287.6 10.9 %all-to-all-start.7 = ((f32[32,1,538]{2,1,0:T(1,128)}), f32[32,1,538]{2,1,0:T(1,128)S(1)}, u32[]{:S(2)}, u32[]{:S(2)}) async-start(f32[32,1,538]{2,1,0:T(1,128)} %broadcast_in_dim.36), calls=%async_computation.8 | async-start | bytes 163840 | tf_op jit(solution)/shard_map/all_to_all | solution.py:27
  298.6 10.0 %all-to-all-done.7 = f32[32,1,538]{2,1,0:T(1,128)S(1)} async-done(((f32[32,1,538]{2,1,0:T(1,128)}), f32[32,1,538]{2,1,0:T(1,128)S(1)}, u32[]{:S(2)}, u32[]{:S(2)}) %all-to-all-start.7) | async-done | bytes 68896 | tf_op jit(solution)/shard_map/all_to_all | solution.py:27
  308.6 0.1 reduce_sum.107
  308.7 0.7 multiply_reduce_fusion.2
  309.4 9.8 %all-reduce.4 = (f32[]{:T(128)}, f32[]{:T(128)}) all-reduce(f32[]{:T(128)} %multiply_reduce_fusion.2, f32[]{:T(128)} %get-tuple-element.14), channel_id=1, replica_groups=mesh['row_0'=4,'row_1'=2,'col_0'=4,'col_1'=8] {'row_0'}, use_global_device_ids=true, to_apply=%region_12.13 | all-reduce | flops 2 | bytes 16 | tf_op jit(solution)/shard_map/psum | solution.py:58
  319.2 3.1 all-reduce.5
  322.3 9.5 %all-reduce.3 = (f32[]{:T(128)}, f32[]{:T(128)}) all-reduce(f32[]{:T(128)} %get-tuple-element.12, f32[]{:T(128)} %get-tuple-element.13), channel_id=1, replica_groups=mesh['row_0'=4,'row_1'=2,'col_0'=4,'col_1'=8] {'col_0'}, use_global_device_ids=true, to_apply=%region_14.15 | all-reduce | flops 2 | bytes 16 | tf_op jit(solution)/shard_map/psum | solution.py:58
  331.8 15.7 %all-reduce.2 = (f32[]{:T(128)}, f32[]{:T(128)}) all-reduce(f32[]{:T(128)} %get-tuple-element.8, f32[]{:T(128)} %get-tuple-element.9), channel_id=1, replica_groups=mesh['row_0'=4,'row_1'=2,'col_0'=4,'col_1'=8] {'col_1'}, use_global_device_ids=true, to_apply=%region_15.16 | all-reduce | flops 2 | bytes 16 | tf_op jit(solution)/shard_map/psum | solution.py:58
  348.2 0.7 fusion.15
  (30 shorter events, 0.2 us)
Async XLA Ops:
  7.2 16.6 %copy-start.1 = (bf16[64,4304]{1,0:T(8,128)(2,1)S(1)}, bf16[64,4304]{1,0:T(8,128)(2,1)}, u32[]{:S(2)}) copy-start(bf16[64,4304]{1,0:T(8,128)(2,1)} %param.9) | copy-start | bytes 1652740
  7.2 135.4 %all-gather.2.cloned.1.call-start = ((), (), s32[]{:S(2)}) async-start(), calls=%async_computation.9 | async-start | bytes 4866048 | tf_op jit(solution)/shard_map/all_gather | solution.py:110
  12.2 57.7 %all-to-all-start.1 = ((bf16[32,36,538]{2,1,0:T(8,128)(2,1)}), bf16[32,36,538]{2,1,0:T(8,128)(2,1)S(1)}, u32[]{:S(2)}, u32[]{:S(2)}) async-start(bf16[32,36,538]{2,1,0:T(8,128)(2,1)} %broadcast_in_dim.32), calls=%async_computation.1 | async-start | bytes 3276800 | tf_op jit(solution)/shard_map/all_to_all | solution.py:27
  69.9 15.2 %all-to-all-start = ((bf16[64,8,538]{2,0,1:T(8,128)(2,1)}), bf16[64,8,538]{2,0,1:T(8,128)(2,1)}, u32[]{:S(2)}, u32[]{:S(2)}) async-start(bf16[64,8,538]{2,0,1:T(8,128)(2,1)} %copy.19), calls=%async_computation | async-start | bytes 1310720 | tf_op jit(solution)/shard_map/all_to_all | solution.py:88
  87.4 33.1 %copy-start = (bf16[64,1152]{1,0:T(8,128)(2,1)S(1)}, bf16[64,1152]{1,0:T(8,128)(2,1)}, u32[]{:S(2)}) copy-start(bf16[64,1152]{1,0:T(8,128)(2,1)} %param.8) | copy-start | bytes 442372
  122.0 20.6 %all-to-all-start.3 = ((bf16[8,64,1152]{2,1,0:T(8,128)(2,1)}), bf16[8,64,1152]{2,1,0:T(8,128)(2,1)S(1)}, u32[]{:S(2)}, u32[]{:S(2)}) async-start(bf16[8,64,1152]{2,1,0:T(8,128)(2,1)} %broadcast_in_dim.33), calls=%async_computation.3 | async-start | bytes 2359296 | tf_op jit(solution)/shard_map/all_to_all | solution.py:27
  126.6 120.1 %reduce-scatter.4.cloned.1.call-start = ((), (), s32[]{:S(2)}) async-start(), calls=%async_computation.10 | async-start | bytes 3686400 | tf_op jit(solution)/shard_map/reduce_scatter | solution.py:48
  142.5 8.2 %copy-start.6 = (bf16[2048,1152]{1,0:T(8,128)(2,1)S(1)}, bf16[2048,1152]{1,0:T(8,128)(2,1)}, u32[]{:S(2)}) copy-start(bf16[2048,1152]{1,0:T(8,128)(2,1)} %all-gather.2.cloned.1.call-done) | copy-start | bytes 14155780
  207.4 68.3 %copy-start.5 = (u32[256]{0:T(256)S(1)}, u32[256]{0:T(256)}, u32[]{:S(2)}) copy-start(u32[256]{0:T(256)} %constant.101) | copy-start | bytes 3076
  211.2 87.3 %copy-start.7 = (f32[36]{0:T(128)S(1)}, f32[36]{0:T(128)}, u32[]{:S(2)}) copy-start(f32[36]{0:T(128)} %param.12) | copy-start | bytes 436
  211.2 97.4 %copy-start.3 = (f32[538]{0:T(1024)S(1)}, f32[538]{0:T(1024)}, u32[]{:S(2)}) copy-start(f32[538]{0:T(1024)} %param.13) | copy-start | bytes 6460
  270.5 7.5 %collective-permute-start = (f32[48,538]{1,0:T(8,128)S(1)}, f32[48,538]{1,0:T(8,128)S(1)}, u32[]{:S(2)}, u32[]{:S(2)}) collective-permute-start(f32[48,538]{1,0:T(8,128)S(1)} %fusion), channel_id=1, source_target_pairs={{0,1},{1,2},{2,3},{3,4},{4,5},{5,6},{6,7},{8,9},{9,10},{10,11},{11... | collective-permute-start | bytes 309896
  273.3 4.6 %collective-permute-start.1 = (f32[36,538]{1,0:T(8,128)S(1)}, f32[36,538]{1,0:T(8,128)S(1)}, u32[]{:S(2)}, u32[]{:S(2)}) collective-permute-start(f32[36,538]{1,0:T(8,128)S(1)} %slice), channel_id=1, source_target_pairs={{0,2},{1,3},{2,4},{3,5},{4,6},{5,7},{8,10},{9,11},{10,12},{11,13},... | collective-permute-start | bytes 232424
  287.6 21.0 %all-to-all-start.7 = ((f32[32,1,538]{2,1,0:T(1,128)}), f32[32,1,538]{2,1,0:T(1,128)S(1)}, u32[]{:S(2)}, u32[]{:S(2)}) async-start(f32[32,1,538]{2,1,0:T(1,128)} %broadcast_in_dim.36), calls=%async_computation.8 | async-start | bytes 163840 | tf_op jit(solution)/shard_map/all_to_all | solution.py:27
  298.6 51.0 %copy-start.4 = (f32[36]{0:T(128)}, f32[36]{0:T(128)S(1)}, u32[]{:S(2)}) copy-start(f32[36]{0:T(128)S(1)} %multiply_add_fusion.2) | copy-start | bytes 436
  308.7 40.9 %copy-start.2 = (f32[538]{0:T(1024)}, f32[538]{0:T(1024)S(1)}, u32[]{:S(2)}) copy-start(f32[538]{0:T(1024)S(1)} %multiply_add_fusion.1) | copy-start | bytes 6460
Sparse Core Ops, SparseCore 0:
  10.6 92.3 all-gather.1
  211.4 35.3 reduce-scatter.3
where the time goes:
time: 358 us
  blocking collectives  156 us (44%)
  waiting for transfers between devices  115 us (32%)
  starting transfers between devices  37.1 us (10%)
  between operations  18.7 us (5%)
  matrix products  18 us (5%)
  local copies, waits for them, and re-layouts  6.69 us (2%)
  other arithmetic  6.23 us (2%)
    all_to_all x3, waiting for transfers between devices, sent_to_all(): return lax.all_to_all(copies, axis, split_axis=0, concat_axis=0, tiled=True)  69 us
    all_to_all x2, blocking collectives, sum_at_owner(): lax.all_to_all(pieces, axis, split_axis=0, concat_axis=0, tiled=True)  65.6 us
    psum x4, blocking collectives, one_axis_at_a_time(): return functools.reduce(lax.psum, axes, array)  38.1 us
    reduce_scatter x1, waiting for transfers between devices, sum_by_axis(): running = lax.psum_scatter(running, axis, scatter_dimension=0, tiled=True)  35.5 us
    all_to_all x2, blocking collectives, sent_to_all(): return lax.all_to_all(copies, axis, split_axis=0, concat_axis=0, tiled=True)  28 us
    all_to_all x3, starting transfers between devices, sent_to_all(): return lax.all_to_all(copies, axis, split_axis=0, concat_axis=0, tiled=True)  27.1 us
    unnamed x1, blocking collectives  23.8 us
    all_to_all x1, waiting for transfers between devices, per_device(): lax.all_to_all(hidden, ROW, split_axis=1, concat_axis=0, tiled=True)  9.71 us
  transfers between devices with their start and end apart: 8, of which 6 were waited for; matrix products, arithmetic and copies ran while one was open for 2% of the time, Pallas kernels for 0%

commit v1 on v0

--- a/solution.py
+++ b/solution.py
@@ -85,7 +85,20 @@
     col_place = lax.axis_index(COL)
     tokens = pooled.shape[0]
     batch_total = tokens * rows_count * cols_count
-    split_hidden = lax.all_to_all(hidden, ROW, split_axis=1, concat_axis=0, tiled=True)
+
+    def pipes_mark(mat, across):
+        x_new = jnp.concatenate(
+            lax.all_to_all(
+                jnp.stack(jnp.split(mat, lax.axis_size(across), 1), axis=0),
+                axis_name=across,
+                split_axis=0,
+                concat_axis=0,
+            ),
+            axis=0,
+        )
+        return x_new
+
+    split_hidden = pipes_mark(hidden, ROW)
     weight_half = weight.astype(jnp.bfloat16)
     partial_proj = lax.dot_general(
         split_hidden,

time: 358 us -> 358 us (level)
  local copies, waits for them, and re-layouts: 6.69 us -> 10.7 us
  waiting for transfers between devices: 115 us -> 111 us
    unnamed x19 -> x26, local copies, waits for them, and re-layouts: 1.01 us -> 5.99 us
    all_to_all x3, waiting for transfers between devices: 69 us -> 65 us  [sent_to_all(): return lax.all_to_all(copies, axis, split_axis=0, concat_axis=0, tiled=True)]
  transfers between devices with their start and end apart: 8 -> 8, of which waited for: 6 -> 6; matrix products, arithmetic and copies ran while one was open for 2% -> 4% of each run, Pallas kernels for 0% -> 0%
where the time goes in v1:
time: 358 us
  blocking collectives  156 us (44%)
  waiting for transfers between devices  111 us (31%)
  starting transfers between devices  37.1 us (10%)
  between operations  18.7 us (5%)
  matrix products  18 us (5%)
  local copies, waits for them, and re-layouts  10.7 us (3%)
  other arithmetic  6.23 us (2%)
    all_to_all x2, blocking collectives, sum_at_owner(): lax.all_to_all(pieces, axis, split_axis=0, concat_axis=0, tiled=True)  65.6 us
    all_to_all x3, waiting for transfers between devices, sent_to_all(): return lax.all_to_all(copies, axis, split_axis=0, concat_axis=0, tiled=True)  65 us
    psum x4, blocking collectives, one_axis_at_a_time(): return functools.reduce(lax.psum, axes, array)  38.1 us
    reduce_scatter x1, waiting for transfers between devices, sum_by_axis(): running = lax.psum_scatter(running, axis, scatter_dimension=0, tiled=True)  35.5 us
    all_to_all x2, blocking collectives, sent_to_all(): return lax.all_to_all(copies, axis, split_axis=0, concat_axis=0, tiled=True)  28.1 us
    all_to_all x3, starting transfers between devices, sent_to_all(): return lax.all_to_all(copies, axis, split_axis=0, concat_axis=0, tiled=True)  27 us
    unnamed x1, blocking collectives  23.7 us
    all_to_all x1, waiting for transfers between devices, pipes_mark(): lax.all_to_all(jnp.stack(jnp.split(mat, lax.axis_size(across), 1), axis=0...  9.71 us
  transfers between devices with their start and end apart: 8, of which 6 were waited for; matrix products, arithmetic and copies ran while one was open for 4% of the time, Pallas kernels for 0%

profile of v1, /device:TPU:2, one launch (start us, length us, event | category | flops | bytes accessed | tf_op | source)
XLA Modules:
  0.0 357.6 jit_solution(7524342107053118465)
XLA Ops:
  7.2 1.1 fusion.8
  8.3 1.7 fusion.9
  10.0 0.9 convert_element_type.22
  10.9 1.3 broadcast_in_dim.32
  12.2 11.5 %all-to-all-start.1 = ((bf16[32,36,538]{2,1,0:T(8,128)(2,1)}), bf16[32,36,538]{2,1,0:T(8,128)(2,1)S(1)}, u32[]{:S(2)}, u32[]{:S(2)}) async-start(bf16[32,36,538]{2,1,0:T(8,128)(2,1)} %broadcast_in_dim.32), calls=%async_computation.1 | async-start | bytes 3276800 | tf_op jit(solution)/shard_map/all_to_all | solution.py:27
  23.8 0.6 bitcast_dynamic-update-slice_fusion.7
  24.4 0.7 bitcast_dynamic-update-slice_fusion.6
  25.1 0.7 bitcast_dynamic-update-slice_fusion.5
  25.8 0.7 bitcast_dynamic-update-slice_fusion.4
  26.6 0.7 bitcast_dynamic-update-slice_fusion.3
  27.3 0.7 bitcast_dynamic-update-slice_fusion.2
  28.0 0.7 bitcast_dynamic-update-slice_fusion.1
  28.7 0.7 bitcast_dynamic-update-slice_fusion
  29.5 40.5 %all-to-all-done.1 = bf16[32,36,538]{2,1,0:T(8,128)(2,1)S(1)} async-done(((bf16[32,36,538]{2,1,0:T(8,128)(2,1)}), bf16[32,36,538]{2,1,0:T(8,128)(2,1)S(1)}, u32[]{:S(2)}, u32[]{:S(2)}) %all-to-all-start.1) | async-done | bytes 1239584 | tf_op jit(solution)/shard_map/all_to_all | solution.py:27
  69.9 4.8 %all-to-all-start = ((bf16[8,64,538]{2,1,0:T(8,128)(2,1)}), bf16[8,64,538]{2,1,0:T(8,128)(2,1)}, u32[]{:S(2)}, u32[]{:S(2)}) async-start(bf16[8,64,538]{2,1,0:T(8,128)(2,1)} %bitcast_dynamic-update-slice_fusion), calls=%async_computation | async-start | bytes 1310720 | tf_op jit(solution)/shard_map/all_to_all | solution.py:91
  74.8 0.6 reshape.73
  75.4 9.7 %all-to-all-done = bf16[8,64,538]{2,1,0:T(8,128)(2,1)} async-done(((bf16[8,64,538]{2,1,0:T(8,128)(2,1)}), bf16[8,64,538]{2,1,0:T(8,128)(2,1)}, u32[]{:S(2)}, u32[]{:S(2)}) %all-to-all-start) | async-done | bytes 550944 | tf_op jit(solution)/shard_map/all_to_all | solution.py:91
  85.1 2.3 fusion.6
  87.5 32.9 %all_to_all.42 = f32[8,64,1152]{2,1,0:T(8,128)S(1)} all-to-all(f32[8,64,1152]{2,1,0:T(8,128)S(1)} %fusion.6), channel_id=1, replica_groups=mesh['row_0'=4,'row_1'=2,'col_0'=4,'col_1'=8] {'row_0','row_1'}, dimensions={0} | all-to-all | bytes 4718592 | tf_op jit(solution)/shard_map/all_to_all | solution.py:42
  120.5 0.1 multiply_reduce_fusion.1
  120.8 1.2 broadcast_in_dim.33
  122.0 4.7 %all-to-all-start.3 = ((bf16[8,64,1152]{2,1,0:T(8,128)(2,1)}), bf16[8,64,1152]{2,1,0:T(8,128)(2,1)S(1)}, u32[]{:S(2)}, u32[]{:S(2)}) async-start(bf16[8,64,1152]{2,1,0:T(8,128)(2,1)} %broadcast_in_dim.33), calls=%async_computation.3 | async-start | bytes 2359296 | tf_op jit(solution)/shard_map/all_to_all | solution.py:27
  128.0 14.5 %all-to-all-done.3 = bf16[8,64,1152]{2,1,0:T(8,128)(2,1)S(1)} async-done(((bf16[8,64,1152]{2,1,0:T(8,128)(2,1)}), bf16[8,64,1152]{2,1,0:T(8,128)(2,1)S(1)}, u32[]{:S(2)}, u32[]{:S(2)}) %all-to-all-start.3) | async-done | bytes 1179680 | tf_op jit(solution)/shard_map/all_to_all | solution.py:27
  142.5 8.2 %fusion.1 = (f32[]{:T(128)}, f32[512,2048]{1,0:T(8,128)S(1)}) fusion(f32[]{:T(128)S(6)} %copy.30, bf16[512,1152]{1,0:T(8,128)(2,1)S(1)} %bitcast.34, bf16[2048,1152]{1,0:T(8,128)(2,1)} %all-gather.2.cloned.1.call-done, f32[]{:T(128)S(6)} %exp.10, s32[2048]{0:T(1024)S(1)} %iota_add_fusion, s32[512]{0:T(512)S(1)} %fusion.21), kind=kOutput, calls=%fused_computation.1 | convolution fusion | flops 2429550592 | bytes 10102796 | tf_op jit(solution)/shard_map/dot_general | solution.py:70
  150.8 3.7 %convolution_multiply_fusion = f32[512,1152]{1,0:T(8,128)S(1)} fusion(bf16[2048,1152]{1,0:T(8,128)(2,1)S(1)} %copy-done.6, f32[512,2048]{1,0:T(8,128)S(1)} %get-tuple-element.15, s32[2048]{0:T(1024)S(1)} %iota_add_fusion, s32[512]{0:T(512)S(1)} %fusion.21, f32[]{:T(128)S(6)} %exp.10), kind=kOutput, calls=%fused_computation.6 | convolution fusion | flops 2425946112 | bytes 11282436 | tf_op jit(solution)/shard_map/dot_general | solution.py:78
  154.5 32.7 %all_to_all.43 = f32[8,64,1152]{2,1,0:T(8,128)S(1)} all-to-all(f32[8,64,1152]{2,1,0:T(8,128)S(1)} %bitcast.33), channel_id=1, replica_groups=mesh['row_0'=4,'row_1'=2,'col_0'=4,'col_1'=8] {'row_0','row_1'}, dimensions={0} | all-to-all | bytes 4718592 | tf_op jit(solution)/shard_map/all_to_all | solution.py:42
  187.3 0.2 multiply_reduce_fusion
  187.7 0.1 broadcast_in_dim.34
  187.8 19.6 %all_to_all.44 = bf16[8,64,1152]{2,1,0:T(8,128)(2,1)S(1)} all-to-all(bf16[8,64,1152]{2,1,0:T(8,128)(2,1)S(1)} %broadcast_in_dim.34), channel_id=1, replica_groups=mesh['row_0'=4,'row_1'=2,'col_0'=4,'col_1'=8] {'row_0','row_1'}, dimensions={0} | all-to-all | bytes 2359296 | tf_op jit(solution)/shard_map/all_to_all | solution.py:27
  207.4 3.8 %convolution_bitcast_fusion = f32[1152,538]{1,0:T(8,128)} fusion(bf16[8,64,1152]{2,1,0:T(8,128)(2,1)S(1)} %all_to_all.44, bf16[8,64,538]{2,1,0:T(8,128)(2,1)} %all-to-all-done), kind=kOutput, calls=%fused_computation.5 | convolution fusion | flops 634650624 | bytes 4209664 | tf_op jit(solution)/shard_map/dot_general | solution.py:136
  211.2 35.5 %reduce-scatter.4.cloned.1.call-done = f32[288,538]{1,0:T(8,128)} async-done(((f32[1152,538]{1,0:T(8,128)}), f32[288,538]{1,0:T(8,128)}) %reduce-scatter.4.cloned.1.call-update) | async-done | bytes 619792 | tf_op jit(solution)/shard_map/reduce_scatter | solution.py:48
  246.7 23.7 %fusion = f32[48,538]{1,0:T(8,128)S(1)} fusion(f32[288,538]{1,0:T(8,128)} %reduce-scatter.4.cloned.1.call-done), kind=kCustom, calls=%all-reduce-scatter | all-reduce-scatter fusion | flops 206593 | bytes 724096
  270.5 2.8 collective-permute-start
  273.3 2.4 collective-permute-start.1
  275.7 0.6 dynamic-slice.4
  277.0 1.0 collective-permute-done.1
  278.0 0.4 concatenate
  278.3 0.1 fusion.12
  278.5 8.5 %all_to_all.45 = f32[8,1,36]{2,1,0:T(1,128)S(1)} all-to-all(f32[8,1,36]{2,1,0:T(1,128)S(1)} %broadcast_in_dim.35), channel_id=1, replica_groups=mesh['row_0'=4,'row_1'=2,'col_0'=4,'col_1'=8] {'row_0','row_1'}, dimensions={0} | all-to-all | bytes 2304 | tf_op jit(solution)/shard_map/all_to_all | solution.py:27
  287.0 0.7 broadcast_in_dim.36
  287.6 10.9 %all-to-all-start.7 = ((f32[32,1,538]{2,1,0:T(1,128)}), f32[32,1,538]{2,1,0:T(1,128)S(1)}, u32[]{:S(2)}, u32[]{:S(2)}) async-start(f32[32,1,538]{2,1,0:T(1,128)} %broadcast_in_dim.36), calls=%async_computation.8 | async-start | bytes 163840 | tf_op jit(solution)/shard_map/all_to_all | solution.py:27
  298.6 10.0 %all-to-all-done.7 = f32[32,1,538]{2,1,0:T(1,128)S(1)} async-done(((f32[32,1,538]{2,1,0:T(1,128)}), f32[32,1,538]{2,1,0:T(1,128)S(1)}, u32[]{:S(2)}, u32[]{:S(2)}) %all-to-all-start.7) | async-done | bytes 68896 | tf_op jit(solution)/shard_map/all_to_all | solution.py:27
  308.7 0.7 multiply_reduce_fusion.2
  309.4 9.8 %all-reduce.4 = (f32[]{:T(128)}, f32[]{:T(128)}) all-reduce(f32[]{:T(128)} %multiply_reduce_fusion.2, f32[]{:T(128)} %get-tuple-element.14), channel_id=1, replica_groups=mesh['row_0'=4,'row_1'=2,'col_0'=4,'col_1'=8] {'row_0'}, use_global_device_ids=true, to_apply=%region_12.13 | all-reduce | flops 2 | bytes 16 | tf_op jit(solution)/shard_map/psum | solution.py:58
  319.2 3.1 all-reduce.5
  322.3 9.5 %all-reduce.3 = (f32[]{:T(128)}, f32[]{:T(128)}) all-reduce(f32[]{:T(128)} %get-tuple-element.12, f32[]{:T(128)} %get-tuple-element.13), channel_id=1, replica_groups=mesh['row_0'=4,'row_1'=2,'col_0'=4,'col_1'=8] {'col_0'}, use_global_device_ids=true, to_apply=%region_14.15 | all-reduce | flops 2 | bytes 16 | tf_op jit(solution)/shard_map/psum | solution.py:58
  331.8 15.7 %all-reduce.2 = (f32[]{:T(128)}, f32[]{:T(128)}) all-reduce(f32[]{:T(128)} %get-tuple-element.8, f32[]{:T(128)} %get-tuple-element.9), channel_id=1, replica_groups=mesh['row_0'=4,'row_1'=2,'col_0'=4,'col_1'=8] {'col_1'}, use_global_device_ids=true, to_apply=%region_15.16 | all-reduce | flops 2 | bytes 16 | tf_op jit(solution)/shard_map/psum | solution.py:58
  348.2 0.7 fusion.13
  (36 shorter events, 0.7 us)
Async XLA Ops:
  7.2 16.6 %copy-start.1 = (bf16[64,4304]{1,0:T(8,128)(2,1)S(1)}, bf16[64,4304]{1,0:T(8,128)(2,1)}, u32[]{:S(2)}) copy-start(bf16[64,4304]{1,0:T(8,128)(2,1)} %param.9) | copy-start | bytes 1652740
  7.2 135.4 %all-gather.2.cloned.1.call-start = ((), (), s32[]{:S(2)}) async-start(), calls=%async_computation.9 | async-start | bytes 4866048 | tf_op jit(solution)/shard_map/all_gather | solution.py:123
  12.2 57.7 %all-to-all-start.1 = ((bf16[32,36,538]{2,1,0:T(8,128)(2,1)}), bf16[32,36,538]{2,1,0:T(8,128)(2,1)S(1)}, u32[]{:S(2)}, u32[]{:S(2)}) async-start(bf16[32,36,538]{2,1,0:T(8,128)(2,1)} %broadcast_in_dim.32), calls=%async_computation.1 | async-start | bytes 3276800 | tf_op jit(solution)/shard_map/all_to_all | solution.py:27
  69.9 15.2 %all-to-all-start = ((bf16[8,64,538]{2,1,0:T(8,128)(2,1)}), bf16[8,64,538]{2,1,0:T(8,128)(2,1)}, u32[]{:S(2)}, u32[]{:S(2)}) async-start(bf16[8,64,538]{2,1,0:T(8,128)(2,1)} %bitcast_dynamic-update-slice_fusion), calls=%async_computation | async-start | bytes 1310720 | tf_op jit(solution)/shard_map/all_to_all | solution.py:91
  87.4 33.1 %copy-start = (bf16[64,1152]{1,0:T(8,128)(2,1)S(1)}, bf16[64,1152]{1,0:T(8,128)(2,1)}, u32[]{:S(2)}) copy-start(bf16[64,1152]{1,0:T(8,128)(2,1)} %param.8) | copy-start | bytes 442372
  122.0 20.6 %all-to-all-start.3 = ((bf16[8,64,1152]{2,1,0:T(8,128)(2,1)}), bf16[8,64,1152]{2,1,0:T(8,128)(2,1)S(1)}, u32[]{:S(2)}, u32[]{:S(2)}) async-start(bf16[8,64,1152]{2,1,0:T(8,128)(2,1)} %broadcast_in_dim.33), calls=%async_computation.3 | async-start | bytes 2359296 | tf_op jit(solution)/shard_map/all_to_all | solution.py:27
  126.6 120.1 %reduce-scatter.4.cloned.1.call-start = ((), (), s32[]{:S(2)}) async-start(), calls=%async_computation.10 | async-start | bytes 3686400 | tf_op jit(solution)/shard_map/reduce_scatter | solution.py:48
  142.5 8.2 %copy-start.6 = (bf16[2048,1152]{1,0:T(8,128)(2,1)S(1)}, bf16[2048,1152]{1,0:T(8,128)(2,1)}, u32[]{:S(2)}) copy-start(bf16[2048,1152]{1,0:T(8,128)(2,1)} %all-gather.2.cloned.1.call-done) | copy-start | bytes 14155780
  207.4 68.3 %copy-start.5 = (u32[256]{0:T(256)S(1)}, u32[256]{0:T(256)}, u32[]{:S(2)}) copy-start(u32[256]{0:T(256)} %constant.101) | copy-start | bytes 3076
  211.2 87.3 %copy-start.7 = (f32[36]{0:T(128)S(1)}, f32[36]{0:T(128)}, u32[]{:S(2)}) copy-start(f32[36]{0:T(128)} %param.12) | copy-start | bytes 436
  211.2 97.4 %copy-start.3 = (f32[538]{0:T(1024)S(1)}, f32[538]{0:T(1024)}, u32[]{:S(2)}) copy-start(f32[538]{0:T(1024)} %param.13) | copy-start | bytes 6460
  270.5 7.5 %collective-permute-start = (f32[48,538]{1,0:T(8,128)S(1)}, f32[48,538]{1,0:T(8,128)S(1)}, u32[]{:S(2)}, u32[]{:S(2)}) collective-permute-start(f32[48,538]{1,0:T(8,128)S(1)} %fusion), channel_id=1, source_target_pairs={{0,1},{1,2},{2,3},{3,4},{4,5},{5,6},{6,7},{8,9},{9,10},{10,11},{11... | collective-permute-start | bytes 309896
  273.3 4.6 %collective-permute-start.1 = (f32[36,538]{1,0:T(8,128)S(1)}, f32[36,538]{1,0:T(8,128)S(1)}, u32[]{:S(2)}, u32[]{:S(2)}) collective-permute-start(f32[36,538]{1,0:T(8,128)S(1)} %slice), channel_id=1, source_target_pairs={{0,2},{1,3},{2,4},{3,5},{4,6},{5,7},{8,10},{9,11},{10,12},{11,13},... | collective-permute-start | bytes 232424
  287.6 20.9 %all-to-all-start.7 = ((f32[32,1,538]{2,1,0:T(1,128)}), f32[32,1,538]{2,1,0:T(1,128)S(1)}, u32[]{:S(2)}, u32[]{:S(2)}) async-start(f32[32,1,538]{2,1,0:T(1,128)} %broadcast_in_dim.36), calls=%async_computation.8 | async-start | bytes 163840 | tf_op jit(solution)/shard_map/all_to_all | solution.py:27
  298.5 51.0 %copy-start.4 = (f32[36]{0:T(128)}, f32[36]{0:T(128)S(1)}, u32[]{:S(2)}) copy-start(f32[36]{0:T(128)S(1)} %multiply_add_fusion.2) | copy-start | bytes 436
  308.7 40.9 %copy-start.2 = (f32[538]{0:T(1024)}, f32[538]{0:T(1024)S(1)}, u32[]{:S(2)}) copy-start(f32[538]{0:T(1024)S(1)} %multiply_add_fusion.1) | copy-start | bytes 6460
Sparse Core Ops, SparseCore 0:
  10.6 92.2 all-gather.1
  211.4 35.3 reduce-scatter.3
